TPU v7x, 32 devices: a whole 2x2x4 slice. The times are simulated.
32 devices in a mesh: by: 4 (over z), bx: 8 (over y, x, core).
Axes of the slice: x: 2, y: 2, z: 4, core: 2. Of those that a mesh axis runs over, the one named last changes fastest.
Arguments:
- wave_fn: float32 [2048, 3, 3, 2048], P('bx', None, None, 'by')
- left_env: float32 [2048, 5, 2048], P('bx')
- mpo_ten: float32 [5, 3, 3, 5], replicated
- right_env: float32 [2048, 5, 2048], P('by')
Outputs:
- output: float32 [2048, 3, 3, 2048], P('bx', None, None, 'by')
All inputs are finite; a program needn't handle non-finite values.
Results may differ from a plain program's by a relative error of at most 0.001.
Values sent between devices are 32-bit elements.
A program may use at most 1 GiB of HBM per device.

v0:
```python
import jax
import jax.numpy as jnp
from jax import lax
from jax.sharding import PartitionSpec as P


def solution(mesh):
    prec_mode = lax.Precision.HIGHEST

    def local_apply(wave_blk, left_rows, mpo_ten, right_rows):
        row_share, mpo_dim, bond_dim = left_rows.shape
        phys_dim = wave_blk.shape[1]
        col_share = wave_blk.shape[3]
        wave_cols = lax.all_gather(wave_blk, 'bx', axis=0, tiled=True)
        stage_one = jnp.dot(left_rows.reshape(row_share * mpo_dim, bond_dim), wave_cols.reshape(bond_dim, phys_dim * phys_dim * col_share), precision=prec_mode, preferred_element_type=jnp.float32)
        stage_one = stage_one.reshape(row_share, mpo_dim, phys_dim, phys_dim, col_share)
        stage_two = jnp.einsum('aupqf,uspv->asvqf', stage_one, mpo_ten, precision=prec_mode, preferred_element_type=jnp.float32)
        stage_three = jnp.einsum('asvqf,vtqr->astrf', stage_two, mpo_ten, precision=prec_mode, preferred_element_type=jnp.float32)
        right_cols = lax.all_to_all(right_rows, 'by', 2, 0, tiled=True)
        part_sum = lax.dot_general(stage_three.reshape(row_share * phys_dim * phys_dim, mpo_dim * col_share), right_cols.reshape(bond_dim, mpo_dim * col_share), (((1,), (1,)), ((), ())), precision=prec_mode, preferred_element_type=jnp.float32)
        part_sum = part_sum.reshape(row_share, phys_dim, phys_dim, bond_dim)
        return lax.psum_scatter(part_sum, 'by', scatter_dimension=3, tiled=True)

    return jax.shard_map(local_apply, mesh=mesh, in_specs=(P('bx', None, None, 'by'), P('bx', None, None), P(), P('by', None, None)), out_specs=P('bx', None, None, 'by'), check_vma=False)
```

profile of v0, /device:TPU:0, one launch (start us, length us, event | category | flops | bytes accessed | tf_op | source)
XLA Modules:
  0.0 1590.3 jit_solution(12163407743894730709)
XLA Ops:
  6.5 0.0 copy-start
  6.5 0.0 all-gather.2.cloned.1.call-start
  6.5 6.1 copy.14
  12.6 0.0 all-gather.2.cloned.1.call-update
  12.6 29.6 %copy.19 = f32[512,5,2048]{0,1,2:T(8,128)} copy(f32[512,5,2048]{2,0,1:T(8,128)} %param.7) | data formatting | bytes 41943040 | tf_op args[3]
  42.2 9.7 all-to-all-start
  51.9 0.0 reduce-scatter.2.cloned.1.call-start
  52.0 0.0 copy-done
  52.0 723.6 %all-to-all-done = f32[512,5,2048]{0,1,2:T(8,128)} async-done(((f32[512,5,2048]{0,1,2:T(8,128)}), f32[512,5,2048]{0,1,2:T(8,128)}, u32[]{:S(2)}, u32[]{:S(2)}) %all-to-all-start) | async-done | bytes 20971552 | tf_op jit(solution)/shard_map/all_to_all | solution.py:19
  775.6 20.1 %copy.20 = f32[512,5,4,512]{0,2,3,1:T(4,128)S(1)} copy(f32[512,5,4,512]{0,1,3,2:T(8,128)} %bitcast.18) | data formatting | bytes 41943040 | tf_op jit(solution)/shard_map/all_to_all | solution.py:19
  795.7 13.5 copy.39
  809.2 0.0 all-gather.2.cloned.1.call-done
  809.2 160.2 %fusion.12 = f32[256,5,3,3,512,1]{4,0,3,2,1,5:T(8,128)} fusion(f32[2048,3,3,512]{0,3,2,1:T(8,128)} %all-gather.2.cloned.1.call-done, f32[256,5,2048]{2,0,1:T(8,128)} %param.5), kind=kOutput, calls=%fused_computation.10 | convolution fusion | flops 144955146240 | bytes 71827456 | tf_op jit(solution)/shard_map/dot_general | solution.py:15
  969.4 73.5 %fusion.4 = f32[256,3,512,3,5,1]{2,4,5,1,3,0:T(8,128)} fusion(f32[256,5,3,3,512,1]{4,0,3,2,1,5:T(8,128)} %fusion.12, f32[5,3,3,5,1,1]{3,2,0,5,1,4:T(4,128)S(1)} %fusion.27), kind=kOutput, calls=%fused_computation.4 | convolution fusion | flops 1061683200 | bytes 47186820 | tf_op jit(solution)/shard_map/aupqf,uspv->asvqf/dot_general | solution.py:17
  1042.9 42.0 %fusion.8 = f32[256,3,3,5,512]{4,3,2,1,0:T(8,128)} fusion(f32[256,3,512,3,5,1]{2,4,5,1,3,0:T(8,128)} %fusion.4, f32[5,3,3,5,1,1]{3,2,1,0,5,4:T(4,128)S(1)} %bitcast.58), kind=kOutput, calls=%fused_computation.8 | convolution fusion | flops 1061683200 | bytes 47186820 | tf_op jit(solution)/shard_map/asvqf,vtqr->astrf/dot_general | solution.py:18
  1084.9 31.2 %copy.18 = f32[256,3,3,5,512]{0,4,3,2,1:T(8,128)} copy(f32[256,3,3,5,512]{4,3,2,1,0:T(8,128)} %fusion.8) | data formatting | bytes 47185920 | tf_op jit(solution)/shard_map/asvqf,vtqr->astrf/transpose | solution.py:18
  1116.1 154.9 %fusion.6 = f32[256,3,3,2048]{3,0,2,1:T(8,128)} fusion(f32[256,3,3,2560]{0,3,2,1:T(8,128)} %bitcast.60, f32[2048,2560]{0,1:T(8,128)} %bitcast.61), kind=kOutput, calls=%fused_computation.6 | convolution fusion | flops 144955146240 | bytes 63438848 | tf_op jit(solution)/shard_map/dot_general | solution.py:20
  1270.9 0.0 reduce-scatter.2.cloned.1.call-update
  1270.9 312.1 %reduce-scatter.2.cloned.1.call-done = f32[256,3,3,512]{3,0,2,1:T(8,128)} async-done(((f32[256,3,3,2048]{3,0,2,1:T(8,128)}), f32[256,3,3,512]{3,0,2,1:T(8,128)}) %reduce-scatter.2.cloned.1.call-update) | async-done | bytes 4718608 | tf_op jit(solution)/shard_map/reduce_scatter | solution.py:22
  (1 shorter events, 0.0 us)
Async XLA Ops:
  6.5 45.4 %copy-start = (f32[5,3,3,5]{3,2,1,0:T(4,128)S(1)}, f32[5,3,3,5]{3,2,1,0:T(4,128)}, u32[]{:S(2)}) copy-start(f32[5,3,3,5]{3,2,1,0:T(4,128)} %param.6) | copy-start | bytes 2704
  6.5 802.6 %all-gather.2.cloned.1.call-start = ((), (), s32[]{:S(2)}) async-start(), calls=%async_computation.2 | async-start | bytes 42467328 | tf_op jit(solution)/shard_map/all_gather | solution.py:14
  42.2 733.4 %all-to-all-start = ((f32[512,5,2048]{0,1,2:T(8,128)}), f32[512,5,2048]{0,1,2:T(8,128)}, u32[]{:S(2)}, u32[]{:S(2)}) async-start(f32[512,5,2048]{0,1,2:T(8,128)} %copy.19), calls=%async_computation | async-start | bytes 67108864 | tf_op jit(solution)/shard_map/all_to_all | solution.py:19
  51.9 1531.1 %reduce-scatter.2.cloned.1.call-start = ((), (), s32[]{:S(2)}) async-start(), calls=%async_computation.3 | async-start | bytes 23592960 | tf_op jit(solution)/shard_map/reduce_scatter | solution.py:22
Sparse Core Ops, SparseCore 0:
  12.7 189.8 all-gather.1
  1271.1 311.9 reduce-scatter.1
where the time goes:
time: 1600 us; the launch traced here: 1590 us
  waiting for transfers between devices  1040 us (65%)
  matrix products  431 us (27%)
  local copies, waits for them, and re-layouts  100 us (6%)
    all_to_all x1, waiting for transfers between devices, local_apply(): right_cols = lax.all_to_all(right_rows, 'by', 2, 0, tiled=True)  724 us
    reduce_scatter x1, waiting for transfers between devices, local_apply(): return lax.psum_scatter(part_sum, 'by', scatter_dimension=3, tiled=True)  312 us
    dot_general x1, matrix products, local_apply(): jnp.dot(left_rows.reshape(row_share * mpo_dim, bond_dim), wave_cols.resha...  160 us
    dot_general x1, matrix products, local_apply(): lax.dot_general(stage_three.reshape(row_share * phys_dim * phys_dim, mpo_...  155 us
    dot_general x1, matrix products, local_apply(): jnp.einsum('aupqf,uspv->asvqf', stage_one, mpo_ten, precision=prec_mode,...  73.5 us
    unnamed x5, local copies, waits for them, and re-layouts  49.1 us
    dot_general x1, matrix products, local_apply(): jnp.einsum('asvqf,vtqr->astrf', stage_two, mpo_ten, precision=prec_mode,...  42 us
  transfers between devices with their start and end apart: 3, of which 2 were waited for; matrix products, arithmetic and copies ran while one was open for 4% of the time, Pallas kernels for 0%

commit v1 on v0

v1 whole, which is shorter than its diff:
```python
import functools

import jax
import jax.numpy as jnp
from jax import lax
from jax.experimental import pallas as pl
from jax.experimental.pallas import tpu as pltpu
from jax.sharding import PartitionSpec as P

HIGH = lax.Precision.HIGHEST
C_CHUNKS = (64, 72, 56, 32, 32)
A_CHUNKS = (40, 48, 56, 56, 56)
W_ROWS = 8


def mpo_kernel(phys, mpo, splat_ref, src_ref, dst_ref, mid_ref):
    rows, cols = src_ref.shape[-2:]
    col_tiles = cols // 128

    def one_tile(step, carry):
        row = pl.multiple_of((step // col_tiles) * 8, 8)
        col = pl.multiple_of((step % col_tiles) * 128, 128)
        tile = (pl.ds(row, 8), pl.ds(col, 128))
        src = [[[src_ref[p * phys + q, r, *tile] for p in range(phys)] for r in range(mpo)] for q in range(phys)]
        for v in range(mpo):
            for t in range(phys):
                acc = [None] * phys
                for q in range(phys):
                    for r in range(mpo):
                        weight = splat_ref[v, t, q, r]
                        for p in range(phys):
                            term = weight * src[q][r][p]
                            acc[p] = term if acc[p] is None else acc[p] + term
                for p in range(phys):
                    mid_ref[p, v, t] = acc[p]
        mid = [[[mid_ref[p, v, t] for t in range(phys)] for v in range(mpo)] for p in range(phys)]
        for u in range(mpo):
            for s in range(phys):
                acc = [None] * phys
                for p in range(phys):
                    for v in range(mpo):
                        weight = splat_ref[u, s, p, v]
                        for t in range(phys):
                            term = weight * mid[p][v][t]
                            acc[t] = term if acc[t] is None else acc[t] + term
                for t in range(phys):
                    dst_ref[u, s * phys + t, *tile] = acc[t]
        return carry

    lax.fori_loop(0, (rows // 8) * col_tiles, one_tile, 0)


def apply_mpo(splat, src, into, start):
    pq, mpo, rows, cols = src.shape
    phys = splat.shape[1]
    total, in_place = into
    tile = W_ROWS
    first = start // tile
    out_shape = jax.ShapeDtypeStruct((mpo, pq, total, cols), jnp.float32)
    in_specs = [
        pl.BlockSpec(splat.shape, lambda i: (0,) * 6),
        pl.BlockSpec((pq, mpo, tile, cols), lambda i: (0, 0, i, 0)),
    ]
    operands = [splat, src]
    aliases = {}
    body = functools.partial(mpo_kernel, phys, mpo)
    if in_place is not None:
        in_specs.append(pl.BlockSpec(memory_space=pl.ANY))
        operands.append(in_place)
        aliases = {2: 0}
        inner = body
        body = lambda splat_ref, src_ref, old_ref, dst_ref, mid_ref: inner(splat_ref, src_ref, dst_ref, mid_ref)
    return pl.pallas_call(
        body,
        grid=(rows // tile,),
        out_shape=out_shape,
        in_specs=in_specs,
        out_specs=pl.BlockSpec((mpo, pq, tile, cols), lambda i: (0, 0, first + i, 0)),
        scratch_shapes=[pltpu.VMEM((phys, mpo, phys, 8, 128), jnp.float32)],
        input_output_aliases=aliases,
        cost_estimate=pl.CostEstimate(flops=rows * cols * 2700, bytes_accessed=rows * cols * 360, transcendentals=0),
        compiler_params=pltpu.CompilerParams(vmem_limit_bytes=60 * 1024 * 1024),
        name="mpo",
    )(*operands)


def copy_kernel(src_ref, dst_ref):
    dst_ref[0] = src_ref[...]


def split_left(left, parts):
    mpo, rows, bond = left.shape
    share = bond // parts
    return pl.pallas_call(
        copy_kernel,
        grid=(parts, mpo),
        out_shape=jax.ShapeDtypeStruct((parts, mpo, rows, share), jnp.float32),
        in_specs=[pl.BlockSpec((1, rows, share), lambda j, u: (u, 0, j))],
        out_specs=pl.BlockSpec((1, 1, rows, share), lambda j, u: (j, u, 0, 0)),
        name="split_left",
    )(left)


def solution(mesh):
    cols_n = mesh.shape['by']
    rows_n = mesh.shape['bx']

    def local_apply(wave_blk, left_rows, mpo_ten, right_rows):
        row_share, mpo, _ = left_rows.shape
        phys = wave_blk.shape[1]
        col_share = wave_blk.shape[3]
        pq = phys * phys
        wave = wave_blk.transpose(1, 2, 0, 3).reshape(pq, row_share, col_share)
        left = split_left(left_rows.transpose(1, 0, 2), rows_n)
        left = lax.all_to_all(left, 'bx', 0, 0, tiled=True)
        right = right_rows.transpose(1, 0, 2).reshape(mpo, col_share, cols_n, col_share)
        right = right.transpose(2, 0, 1, 3)
        splat = jnp.broadcast_to(mpo_ten[..., None, None], mpo_ten.shape + (8, 128))

        starts = [sum(C_CHUNKS[:i]) for i in range(len(C_CHUNKS))]
        gathered = []
        for start, rows in zip(starts, C_CHUNKS):
            gathered.append(lax.all_gather(wave[:, start:start + rows], 'by', axis=0, tiled=False))

        mid = None
        for i, start in enumerate(starts):
            mixed = lax.dot_general(gathered[i], right, (((0, 3), (0, 3)), ((), ())), precision=HIGH, preferred_element_type=jnp.float32)
            mid = apply_mpo(splat, mixed.transpose(0, 2, 1, 3), (row_share, mid), start)

        outs = []
        done = 0
        for rows in A_CHUNKS:
            part = lax.dot_general(left[:, :, done:done + rows], mid, (((1, 3), (0, 2)), ((), ())), precision=HIGH, preferred_element_type=jnp.float32)
            part = part.transpose(2, 0, 1, 3).reshape(pq, rows_n * rows, col_share)
            outs.append(lax.psum_scatter(part, 'bx', scatter_dimension=1, tiled=True))
            done += rows
        out = jnp.concatenate(outs, axis=1)
        return out.reshape(phys, phys, row_share, col_share).transpose(2, 0, 1, 3)

    return jax.shard_map(local_apply, mesh=mesh, in_specs=(P('bx', None, None, 'by'), P('bx', None, None), P(), P('by', None, None)), out_specs=P('bx', None, None, 'by'), check_vma=False)
```

time: 1600 us -> 872 us (0.55)
  waiting for transfers between devices: 1040 us -> 369 us
  Pallas kernels: 0 us -> 86.1 us
  local copies, waits for them, and re-layouts: 100 us -> 21.7 us
  matrix products: 431 us -> 368 us
    all_to_all x1, waiting for transfers between devices: 724 us -> 0.01 us  [local_apply(): left = lax.all_to_all(left, 'bx', 0, 0, tiled=True)]
    all_gather x1 -> x5, waiting for transfers between devices: 0.01 us -> 184 us  [local_apply(): lax.all_gather(wave[:, start:start + rows], 'by', axis=0, tiled=False)]
    reduce_scatter x1 -> x5, waiting for transfers between devices: 312 us -> 184 us  [local_apply(): outs.append(lax.psum_scatter(part, 'bx', scatter_dimension=1, tiled=True))]
    pallas_call x0 -> x6, Pallas kernels: none -> 86.1 us  [the longest x5 62.4 us: apply_mpo(): pl.pallas_call(body, grid=(rows // tile,), out_shape=out_shape, in_specs=...]
    dot_general x4 -> x10, matrix products: 431 us -> 368 us  [the longest x5 186 us: local_apply(): lax.dot_general(left[:, :, done:done + rows], mid, (((1, 3), (0, 2)), (()...]
    unnamed x5 -> x6, local copies, waits for them, and re-layouts: 49.1 us -> 8.66 us
    transpose x1 -> x0, local copies, waits for them, and re-layouts: 31.2 us -> none  [local_apply(): jnp.einsum('asvqf,vtqr->astrf', stage_two, mpo_ten, precision=prec_mode,...]
    all_to_all x1 -> x0, local copies, waits for them, and re-layouts: 20.1 us -> none  [local_apply(): right_cols = lax.all_to_all(right_rows, 'by', 2, 0, tiled=True)]
  transfers between devices with their start and end apart: 3 -> 11, of which waited for: 2 -> 8; matrix products, arithmetic and copies ran while one was open for 4% -> 41% of each run, Pallas kernels for 0% -> 10%
where the time goes in v1:
time: 872 us; the launch traced here: 865 us
  waiting for transfers between devices  369 us (42%)
  matrix products  368 us (42%)
  Pallas kernels  86.1 us (10%)
  local copies, waits for them, and re-layouts  21.7 us (2%)
  between operations  13.7 us (2%)
    dot_general x5, matrix products, local_apply(): lax.dot_general(left[:, :, done:done + rows], mid, (((1, 3), (0, 2)), (()...  186 us
    all_gather x5, waiting for transfers between devices, local_apply(): lax.all_gather(wave[:, start:start + rows], 'by', axis=0, tiled=False)  184 us
    reduce_scatter x5, waiting for transfers between devices, local_apply(): outs.append(lax.psum_scatter(part, 'bx', scatter_dimension=1, tiled=True))  184 us
    dot_general x5, matrix products, local_apply(): lax.dot_general(gathered[i], right, (((0, 3), (0, 3)), ((), ())), precisi...  182 us
    pallas_call x5, Pallas kernels, apply_mpo(): pl.pallas_call(body, grid=(rows // tile,), out_shape=out_shape, in_specs=...  62.4 us
    pallas_call x1, Pallas kernels, split_left(): pl.pallas_call(copy_kernel, grid=(parts, mpo), out_shape=jax.ShapeDtypeSt...  23.7 us
  transfers between devices with their start and end apart: 11, of which 8 were waited for; matrix products, arithmetic and copies ran while one was open for 41% of the time, Pallas kernels for 10%

profile of v1, /device:TPU:0, one launch (start us, length us, event | category | flops | bytes accessed | tf_op | source)
XLA Modules:
  0.0 864.6 jit_solution(8792480210012696291)
XLA Ops:
  6.5 2.4 fusion.40
  9.0 0.0 all-gather.11.cloned.1.call-start
  9.0 0.7 all-gather.11.cloned.1.call-update
  9.7 0.0 all-gather.15.cloned.1.call-start
  9.8 2.3 slice.42
  12.1 0.0 all-gather.15.cloned.1.call-update
  12.1 0.0 all-gather.19.cloned.1.call-start
  12.1 2.4 slice.44
  14.5 0.0 all-gather.19.cloned.1.call-update
  14.5 0.0 all-gather.17.cloned.1.call-start
  14.6 2.5 slice.43
  17.1 23.7 %split_left.1 = f32[8,5,256,256]{3,2,1,0:T(8,128)} custom-call(f32[5,256,2048]{2,1,0:T(8,128)} %bitcast.151), custom_call_target="tpu_custom_call" | custom-call | tf_op jit(solution)/shard_map/split_left/pallas_call | solution.py:94
  40.8 5.2 all-to-all-start
  46.0 0.0 reduce-scatter.6.cloned.1.call-start
  46.0 15.8 %all-gather.13.cloned.1.call-done = f32[36,32,512]{2,1,0:T(8,128)} async-done(((f32[9,32,512]{2,1,0:T(8,128)}), f32[36,32,512]{2,1,0:T(8,128)}) %all-gather.13.cloned.1.call-update) | async-done | bytes 2359312 | tf_op jit(solution)/shard_map/all_gather | solution.py:123
  61.8 25.7 %fusion.37.src_ref = f32[9,5,32,512]{3,2,1,0:T(8,128)} fusion(f32[5,64,4,8,512]{4,3,2,1,0:T(8,128)} %bitcast.160, f32[4,9,32,512,1]{3,2,1,0,4:T(8,128)} %bitcast.168), kind=kOutput, calls=%fused_computation.34 | convolution fusion | flops 18119393280 | bytes 26279936 | tf_op jit(solution)/shard_map/dot_general | solution.py:127
  87.5 24.7 %all-gather.11.cloned.1.call-done = f32[36,32,512]{2,1,0:T(8,128)} async-done(((f32[9,32,512]{2,1,0:T(8,128)}), f32[36,32,512]{2,1,0:T(8,128)}) %all-gather.11.cloned.1.call-update) | async-done | bytes 2359312 | tf_op jit(solution)/shard_map/all_gather | solution.py:123
  112.2 25.7 %fusion.34.src_ref = f32[9,5,32,512]{3,2,1,0:T(8,128)} fusion(f32[5,64,4,8,512]{4,3,2,1,0:T(8,128)} %bitcast.161, f32[4,9,32,512,1]{3,2,1,0,4:T(8,128)} %bitcast.169), kind=kOutput, calls=%fused_computation.33 | convolution fusion | flops 18119393280 | bytes 26279936 | tf_op jit(solution)/shard_map/dot_general | solution.py:127
  137.8 54.4 %all-gather.15.cloned.1.call-done = f32[36,56,512]{2,1,0:T(8,128)} async-done(((f32[9,56,512]{2,1,0:T(8,128)}), f32[36,56,512]{2,1,0:T(8,128)}) %all-gather.15.cloned.1.call-update) | async-done | bytes 4128784 | tf_op jit(solution)/shard_map/all_gather | solution.py:123
  192.2 39.5 %fusion.29.src_ref = f32[9,5,56,512]{3,2,1,0:T(8,128)} fusion(f32[5,64,4,8,512]{4,3,2,1,0:T(8,128)} %bitcast.162, f32[4,9,56,512,1]{3,2,1,0,4:T(8,128)} %bitcast.167), kind=kOutput, calls=%fused_computation.26 | convolution fusion | flops 31708938240 | bytes 30261248 | tf_op jit(solution)/shard_map/dot_general | solution.py:127
  231.7 49.9 %all-gather.19.cloned.1.call-done = f32[36,64,512]{2,1,0:T(8,128)} async-done(((f32[9,64,512]{2,1,0:T(8,128)}), f32[36,64,512]{2,1,0:T(8,128)}) %all-gather.19.cloned.1.call-update) | async-done | bytes 4718608 | tf_op jit(solution)/shard_map/all_gather | solution.py:123
  281.6 43.3 %fusion.26.src_ref = f32[9,5,64,512]{3,2,1,0:T(8,128)} fusion(f32[5,64,4,8,512]{4,3,2,1,0:T(8,128)} %bitcast.163, f32[4,9,64,512,1]{3,2,1,0,4:T(8,128)} %bitcast.166), kind=kOutput, calls=%fused_computation.25 | convolution fusion | flops 36238786560 | bytes 31588352 | tf_op jit(solution)/shard_map/dot_general | solution.py:127
  324.9 1.2 broadcast_in_dim.2.splat_ref
  326.1 15.0 %mpo.5.old_ref = f32[5,9,256,512]{3,2,1,0:T(8,128)} custom-call(f32[5,3,3,5,8,128]{5,4,3,2,1,0:T(8,128)} %broadcast_in_dim.2.splat_ref, f32[9,5,64,512]{3,2,1,0:T(8,128)} %fusion.26.src_ref), custom_call_target="tpu_custom_call" | custom-call | flops 88473600 | bytes 11796480 | tf_op jit(solution)/shard_map/mpo/pallas_call | solution.py:73
  341.0 39.5 %all-gather.17.cloned.1.call-done = f32[36,72,512]{2,1,0:T(8,128)} async-done(((f32[9,72,512]{2,1,0:T(8,128)}), f32[36,72,512]{2,1,0:T(8,128)}) %all-gather.17.cloned.1.call-update) | async-done | bytes 5308432 | tf_op jit(solution)/shard_map/all_gather | solution.py:123
  380.5 47.9 %fusion.23.src_ref = f32[9,5,72,512]{3,2,1,0:T(8,128)} fusion(f32[5,64,4,8,512]{4,3,2,1,0:T(8,128)} %bitcast.164, f32[4,9,72,512,1]{3,2,1,0,4:T(8,128)} %bitcast.165), kind=kOutput, calls=%fused_computation.24 | convolution fusion | flops 40768634880 | bytes 32915456 | tf_op jit(solution)/shard_map/dot_general | solution.py:127
  428.4 16.5 %mpo.6.old_ref = f32[5,9,256,512]{3,2,1,0:T(8,128)} custom-call(f32[5,3,3,5,8,128]{5,4,3,2,1,0:T(8,128)} %broadcast_in_dim.2.splat_ref, f32[9,5,72,512]{3,2,1,0:T(8,128)} %fusion.23.src_ref, f32[5,9,256,512]{3,2,1,0:T(8,128)} %mpo.5.old_ref), custom_call_target="tpu_custom_call", output_to_operand_aliasing={{}: (2, {})} | custom-call | flops 99532800 | bytes 13271040 | tf_op jit(solution)/shard_map/mpo/pallas_call | solution.py:73
  444.9 13.7 %mpo.7.old_ref = f32[5,9,256,512]{3,2,1,0:T(8,128)} custom-call(f32[5,3,3,5,8,128]{5,4,3,2,1,0:T(8,128)} %broadcast_in_dim.2.splat_ref, f32[9,5,56,512]{3,2,1,0:T(8,128)} %fusion.29.src_ref, f32[5,9,256,512]{3,2,1,0:T(8,128)} %mpo.6.old_ref), custom_call_target="tpu_custom_call", output_to_operand_aliasing={{}: (2, {})} | custom-call | flops 77414400 | bytes 10321920 | tf_op jit(solution)/shard_map/mpo/pallas_call | solution.py:73
  458.7 8.6 mpo.8.old_ref
  467.3 8.6 mpo.9
  475.9 29.7 %fusion.13 = f32[9,512,8,40,1]{1,3,4,2,0:T(8,128)} fusion(f32[8,5,256,256]{3,2,1,0:T(8,128)} %all-to-all-done, f32[5,9,256,512]{3,2,1,0:T(8,128)} %mpo.9), kind=kOutput, calls=%fused_computation.14 | convolution fusion | flops 22649241600 | bytes 31129600 | tf_op jit(solution)/shard_map/dot_general | solution.py:133
  505.6 0.0 reduce-scatter.8.cloned.1.call-start
  505.7 35.0 %fusion.11 = f32[9,512,8,48,1]{1,3,4,2,0:T(8,128)} fusion(f32[8,5,256,256]{3,2,1,0:T(8,128)} %all-to-all-done, f32[5,9,256,512]{3,2,1,0:T(8,128)} %mpo.9), kind=kOutput, calls=%fused_computation.12 | convolution fusion | flops 27179089920 | bytes 32636928 | tf_op jit(solution)/shard_map/dot_general | solution.py:133
  540.7 0.0 reduce-scatter.10.cloned.1.call-start
  540.8 40.5 %fusion.9 = f32[9,512,8,56,1]{1,3,4,2,0:T(8,128)} fusion(f32[8,5,256,256]{3,2,1,0:T(8,128)} %all-to-all-done, f32[5,9,256,512]{3,2,1,0:T(8,128)} %mpo.9), kind=kOutput, calls=%fused_computation.10 | convolution fusion | flops 31708938240 | bytes 34144256 | tf_op jit(solution)/shard_map/dot_general | solution.py:133
  581.3 0.0 reduce-scatter.12.cloned.1.call-start
  581.4 40.7 %fusion.7 = f32[9,512,8,56,1]{1,3,4,2,0:T(8,128)} fusion(f32[8,5,256,256]{3,2,1,0:T(8,128)} %all-to-all-done, f32[5,9,256,512]{3,2,1,0:T(8,128)} %mpo.9), kind=kOutput, calls=%fused_computation.8 | convolution fusion | flops 31708938240 | bytes 34144256 | tf_op jit(solution)/shard_map/dot_general | solution.py:133
  622.1 0.0 reduce-scatter.14.cloned.1.call-start
  622.2 40.4 %fusion.5 = f32[9,512,8,56,1]{1,3,4,2,0:T(8,128)} fusion(f32[8,5,256,256]{3,2,1,0:T(8,128)} %all-to-all-done, f32[5,9,256,512]{3,2,1,0:T(8,128)} %mpo.9), kind=kOutput, calls=%fused_computation.6 | convolution fusion | flops 31708938240 | bytes 34144256 | tf_op jit(solution)/shard_map/dot_general | solution.py:133
  662.6 0.0 reduce-scatter.6.cloned.1.call-done
  662.6 2.0 constant_dynamic-update-slice_fusion.4
  664.7 2.1 constant_dynamic-update-slice_fusion.3
  666.8 40.0 %reduce-scatter.10.cloned.1.call-done = f32[9,56,512]{2,1,0:T(8,128)} async-done(((f32[9,448,512]{2,1,0:T(8,128)}), f32[9,56,512]{2,1,0:T(8,128)}) %reduce-scatter.10.cloned.1.call-update) | async-done | bytes 1032208 | tf_op jit(solution)/shard_map/reduce_scatter | solution.py:135
  706.8 2.2 constant_dynamic-update-slice_fusion.2
  709.0 72.1 %reduce-scatter.12.cloned.1.call-done = f32[9,56,512]{2,1,0:T(8,128)} async-done(((f32[9,448,512]{2,1,0:T(8,128)}), f32[9,56,512]{2,1,0:T(8,128)}) %reduce-scatter.12.cloned.1.call-update) | async-done | bytes 1032208 | tf_op jit(solution)/shard_map/reduce_scatter | solution.py:135
  781.1 2.2 constant_dynamic-update-slice_fusion.1
  783.4 71.9 %reduce-scatter.14.cloned.1.call-done = f32[9,56,512]{2,1,0:T(8,128)} async-done(((f32[9,448,512]{2,1,0:T(8,128)}), f32[9,56,512]{2,1,0:T(8,128)}) %reduce-scatter.14.cloned.1.call-update) | async-done | bytes 1032208 | tf_op jit(solution)/shard_map/reduce_scatter | solution.py:135
  855.3 2.2 constant_dynamic-update-slice_fusion
  (12 shorter events, 0.1 us)
Async XLA Ops:
  6.5 55.3 %all-gather.13.cloned.1.call-start = ((), (), s32[]{:S(2)}) async-start(), calls=%async_computation.12 | async-start | bytes 2949120 | tf_op jit(solution)/shard_map/all_gather | solution.py:123
  9.0 103.2 %all-gather.11.cloned.1.call-start = ((), (), s32[]{:S(2)}) async-start(), calls=%async_computation.11 | async-start | bytes 2949120 | tf_op jit(solution)/shard_map/all_gather | solution.py:123
  9.7 182.5 %all-gather.15.cloned.1.call-start = ((), (), s32[]{:S(2)}) async-start(), calls=%async_computation.13 | async-start | bytes 5160960 | tf_op jit(solution)/shard_map/all_gather | solution.py:123
  12.1 269.5 %all-gather.19.cloned.1.call-start = ((), (), s32[]{:S(2)}) async-start(), calls=%async_computation.15 | async-start | bytes 5898240 | tf_op jit(solution)/shard_map/all_gather | solution.py:123
  14.5 366.0 %all-gather.17.cloned.1.call-start = ((), (), s32[]{:S(2)}) async-start(), calls=%async_computation.14 | async-start | bytes 6635520 | tf_op jit(solution)/shard_map/all_gather | solution.py:123
  40.8 435.0 %all-to-all-start = ((f32[8,5,256,256]{3,2,1,0:T(8,128)}), f32[8,5,256,256]{3,2,1,0:T(8,128)}, u32[]{:S(2)}, u32[]{:S(2)}) async-start(f32[8,5,256,256]{3,2,1,0:T(8,128)} %split_left.1), calls=%async_computation | async-start | bytes 20971520 | tf_op jit(solution)/shard_map/all_to_all | solution.py:115
  46.0 616.6 %reduce-scatter.6.cloned.1.call-start = ((), (), s32[]{:S(2)}) async-start(), calls=%async_computation.6 | async-start | bytes 6635520 | tf_op jit(solution)/shard_map/reduce_scatter | solution.py:135
  281.6 43.3 %copy-start = (f32[5,3,3,5]{3,2,1,0:T(4,128)S(1)}, f32[5,3,3,5]{3,2,1,0:T(4,128)}, u32[]{:S(2)}) copy-start(f32[5,3,3,5]{3,2,1,0:T(4,128)} %param.6) | copy-start | bytes 2704
  505.6 159.0 %reduce-scatter.8.cloned.1.call-start = ((), (), s32[]{:S(2)}) async-start(), calls=%async_computation.7 | async-start | bytes 7962624 | tf_op jit(solution)/shard_map/reduce_scatter | solution.py:135
  540.7 166.1 %reduce-scatter.10.cloned.1.call-start = ((), (), s32[]{:S(2)}) async-start(), calls=%async_computation.8 | async-start | bytes 9289728 | tf_op jit(solution)/shard_map/reduce_scatter | solution.py:135
  581.3 199.8 %reduce-scatter.12.cloned.1.call-start = ((), (), s32[]{:S(2)}) async-start(), calls=%async_computation.9 | async-start | bytes 9289728 | tf_op jit(solution)/shard_map/reduce_scatter | solution.py:135
  622.1 233.2 %reduce-scatter.14.cloned.1.call-start = ((), (), s32[]{:S(2)}) async-start(), calls=%async_computation.10 | async-start | bytes 9289728 | tf_op jit(solution)/shard_map/reduce_scatter | solution.py:135
Sparse Core Ops, SparseCore 0:
  9.1 52.6 all-gather.12
  63.4 48.7 all-gather.10
  113.8 78.4 all-gather.14
  193.6 87.8 all-gather.18
  283.0 97.5 all-gather.16
  505.7 57.8 reduce-scatter.5
  567.1 65.3 reduce-scatter.7
  636.1 70.6 reduce-scatter.9
  710.5 70.6 reduce-scatter.11
  784.6 70.6 reduce-scatter.13
